TPU v7x, 8 devices: a whole 2x2x1 slice. The times are simulated.
8 devices in a mesh: stage: 2 (over z, y), data: 4 (over x, core).
Axes of the slice: x: 2, y: 2, z: 1, core: 2. Of those that a mesh axis runs over, the one named last changes fastest.
Arguments:
- x_in: bfloat16 [24, 8192, 256], P(None, 'data')
- targets: bfloat16 [24, 8192, 256], P(None, 'data')
- w1_bf: bfloat16 [2, 2, 2, 256, 1024], P('stage')
- w2_bf: bfloat16 [2, 2, 2, 1024, 256], P('stage')
- w_master: float32 [2, 2, 2, 524288], P('stage', None, None, 'data')
- m_state: float32 [2, 2, 2, 524288], P('stage', None, None, 'data')
- v_state: float32 [2, 2, 2, 524288], P('stage', None, None, 'data')
Outputs:
- output 1: bfloat16 [2, 2, 2, 256, 1024], P('stage')
- output 2: bfloat16 [2, 2, 2, 1024, 256], P('stage')
- output 3: float32 [2, 2, 2, 524288], P('stage', None, None, 'data')
- output 4: float32 [2, 2, 2, 524288], P('stage', None, None, 'data')
- output 5: float32 [2, 2, 2, 524288], P('stage', None, None, 'data')
- output 6: float32 [], replicated
All inputs are finite; a program needn't handle non-finite values.
Results may differ from a plain program's by a relative error of at most 0.001.
Values are sent between devices in bfloat16 or wider.
A program may use at most 1 GiB of HBM per device.

v0:
```python
import math
import jax
import jax.numpy as jnp
from jax import lax
from jax.sharding import PartitionSpec as P

BETA_ONE = 0.9
BETA_TWO = 0.999
ADAM_EPS = 1e-8
WEIGHT_DECAY = 0.1
ADAM_STEP = 1000


def gelu_tanh(pre_act):
    return jax.nn.gelu(pre_act, approximate=True)


def block_forward(h_in, w_one, w_two):
    pre_act = jnp.dot(h_in, w_one, preferred_element_type=jnp.float32)
    act_bf = gelu_tanh(pre_act).astype(jnp.bfloat16)
    out_val = h_in.astype(jnp.float32) + jnp.dot(act_bf, w_two, preferred_element_type=jnp.float32)
    return out_val.astype(jnp.bfloat16)


def block_backward(h_in, grad_out, w_one, w_two):
    pre_act = jnp.dot(h_in, w_one, preferred_element_type=jnp.float32)
    act_val, gelu_pull = jax.vjp(gelu_tanh, pre_act)
    grad_act = jnp.einsum("td,fd->tf", grad_out, w_two, preferred_element_type=jnp.float32)
    grad_pre = gelu_pull(grad_act)[0].astype(jnp.bfloat16)
    back_val = jnp.einsum("tf,df->td", grad_pre, w_one, preferred_element_type=jnp.float32)
    grad_in = (grad_out.astype(jnp.float32) + back_val).astype(jnp.bfloat16)
    grad_one = jnp.einsum("td,tf->df", h_in, grad_pre, preferred_element_type=jnp.float32)
    grad_two = jnp.einsum("tf,td->fd", act_val.astype(jnp.bfloat16), grad_out, preferred_element_type=jnp.float32)
    return grad_in, grad_one, grad_two


def adam_update(w_old, m_old, v_old, grad_val, clip_factor, learn_rate):
    grad_clip = clip_factor * grad_val
    m_new = BETA_ONE * m_old + (1.0 - BETA_ONE) * grad_clip
    v_new = BETA_TWO * v_old + (1.0 - BETA_TWO) * grad_clip * grad_clip
    m_hat = m_new / (1.0 - BETA_ONE ** ADAM_STEP)
    v_hat = v_new / (1.0 - BETA_TWO ** ADAM_STEP)
    w_new = w_old - learn_rate * (m_hat / (jnp.sqrt(v_hat) + ADAM_EPS) + WEIGHT_DECAY * w_old)
    return w_new, m_new, v_new


def item_coords(item_idx, n_stage, backward):
    group_idx = item_idx // (2 * n_stage)
    within = item_idx % (2 * n_stage)
    half_idx = within // n_stage
    if backward:
        half_idx = 1 - half_idx
    return half_idx, group_idx * n_stage + within % n_stage


def run_stack(x_loc, t_loc, w_ones, w_twos, n_stage, n_tokens):
    stage_idx = lax.axis_index("stage")
    n_micro, n_tok, d_model = x_loc.shape
    n_blk, d_ff = w_ones.shape[1], w_ones.shape[3]
    n_items = 2 * n_micro
    n_ticks = n_items + n_stage - 1
    fwd_perm = [(src, (src + 1) % n_stage) for src in range(n_stage)]
    bwd_perm = [(src, (src - 1) % n_stage) for src in range(n_stage)]

    def fwd_tick(tick_idx, state_carry):
        recv_act, saved_in, seed_buf, loss_acc = state_carry
        item_idx = tick_idx - stage_idx
        active = (item_idx >= 0) & (item_idx < n_items)
        half_idx, micro_idx = item_coords(jnp.clip(item_idx, 0, n_items - 1), n_stage, False)
        slot_idx = jnp.where(active, micro_idx, n_micro)
        x_mb = lax.dynamic_index_in_dim(x_loc, micro_idx, 0, keepdims=False)
        h_cur = jnp.where((half_idx == 0) & (stage_idx == 0), x_mb, recv_act)
        half_one = lax.dynamic_index_in_dim(w_ones, half_idx, 0, keepdims=False)
        half_two = lax.dynamic_index_in_dim(w_twos, half_idx, 0, keepdims=False)
        for block_idx in range(n_blk):
            saved_in = lax.dynamic_update_slice(saved_in, h_cur[None, None, None], (half_idx, slot_idx, block_idx, 0, 0))
            h_cur = block_forward(h_cur, half_one[block_idx], half_two[block_idx])
        is_last = active & (half_idx == 1) & (stage_idx == n_stage - 1)
        t_mb = lax.dynamic_index_in_dim(t_loc, micro_idx, 0, keepdims=False)
        residual = h_cur.astype(jnp.float32) - t_mb.astype(jnp.float32)
        loss_acc = loss_acc + jnp.where(is_last, 0.5 * jnp.sum(residual * residual), 0.0)
        seed_slot = jnp.where(is_last, micro_idx, n_micro)
        seed_buf = lax.dynamic_update_slice(seed_buf, (residual / n_tokens).astype(jnp.bfloat16)[None], (seed_slot, 0, 0))
        recv_act = lax.ppermute(h_cur, "stage", fwd_perm)
        return recv_act, saved_in, seed_buf, loss_acc

    fwd_start = (jnp.zeros((n_tok, d_model), jnp.bfloat16), jnp.zeros((2, n_micro + 1, n_blk, n_tok, d_model), jnp.bfloat16), jnp.zeros((n_micro + 1, n_tok, d_model), jnp.bfloat16), jnp.zeros((), jnp.float32))
    fwd_out = lax.fori_loop(0, n_ticks, fwd_tick, fwd_start)
    saved_in, seed_buf, loss_acc = fwd_out[1], fwd_out[2], fwd_out[3]

    def bwd_tick(tick_idx, state_carry):
        recv_grad, acc_one, acc_two = state_carry
        item_idx = tick_idx - (n_stage - 1 - stage_idx)
        active = (item_idx >= 0) & (item_idx < n_items)
        half_idx, micro_idx = item_coords(jnp.clip(item_idx, 0, n_items - 1), n_stage, True)
        seed_mb = lax.dynamic_index_in_dim(seed_buf, micro_idx, 0, keepdims=False)
        is_seed = (half_idx == 1) & (stage_idx == n_stage - 1)
        grad_cur = jnp.where(is_seed, seed_mb, recv_grad)
        grad_cur = jnp.where(active, grad_cur, jnp.zeros_like(grad_cur))
        half_one = lax.dynamic_index_in_dim(w_ones, half_idx, 0, keepdims=False)
        half_two = lax.dynamic_index_in_dim(w_twos, half_idx, 0, keepdims=False)
        saved_mb = lax.dynamic_slice(saved_in, (half_idx, micro_idx, 0, 0, 0), (1, 1, n_blk, n_tok, d_model))[0, 0]
        for block_idx in reversed(range(n_blk)):
            grad_cur, grad_one, grad_two = block_backward(saved_mb[block_idx], grad_cur, half_one[block_idx], half_two[block_idx])
            old_one = lax.dynamic_slice(acc_one, (half_idx, block_idx, 0, 0), (1, 1, d_model, d_ff))
            acc_one = lax.dynamic_update_slice(acc_one, old_one + grad_one[None, None], (half_idx, block_idx, 0, 0))
            old_two = lax.dynamic_slice(acc_two, (half_idx, block_idx, 0, 0), (1, 1, d_ff, d_model))
            acc_two = lax.dynamic_update_slice(acc_two, old_two + grad_two[None, None], (half_idx, block_idx, 0, 0))
        recv_grad = lax.ppermute(grad_cur, "stage", bwd_perm)
        return recv_grad, acc_one, acc_two

    bwd_start = (jnp.zeros((n_tok, d_model), jnp.bfloat16), jnp.zeros((2, n_blk, d_model, d_ff), jnp.float32), jnp.zeros((2, n_blk, d_ff, d_model), jnp.float32))
    bwd_out = lax.fori_loop(0, n_ticks, bwd_tick, bwd_start)
    return bwd_out[1], bwd_out[2], loss_acc


def solution(mesh):
    n_stage = mesh.shape["stage"]
    n_data = mesh.shape["data"]

    def device_step(x_loc, t_loc, w1_loc, w2_loc, wm_loc, m_loc, v_loc):
        n_micro, n_tok, d_model = x_loc.shape
        n_blk, d_ff = w1_loc.shape[2], w1_loc.shape[4]
        n_tokens = n_micro * n_tok * n_data
        n_blocks = 2 * n_stage * n_blk
        tau_clip = 0.3 * d_model * math.sqrt(n_blocks * (3.0 / n_tokens + 0.008))
        learn_rate = 0.1 / math.sqrt(4.0 * d_model * n_blocks)
        acc_one, acc_two, loss_acc = run_stack(x_loc, t_loc, w1_loc[0], w2_loc[0], n_stage, n_tokens)
        grad_flat = jnp.concatenate([acc_one.reshape(2, n_blk, -1), acc_two.reshape(2, n_blk, -1)], axis=-1)
        grad_shard = lax.psum_scatter(grad_flat, "data", scatter_dimension=2, tiled=True)
        grad_norm = jnp.sqrt(lax.psum(jnp.sum(grad_shard * grad_shard), ("stage", "data")))
        clip_factor = jnp.minimum(1.0, tau_clip / grad_norm)
        w_new, m_new, v_new = adam_update(wm_loc[0], m_loc[0], v_loc[0], grad_shard, clip_factor, learn_rate)
        w_full = lax.all_gather(w_new.astype(jnp.bfloat16), "data", axis=2, tiled=True)
        split_at = d_model * d_ff
        w1_new = w_full[:, :, :split_at].reshape(1, 2, n_blk, d_model, d_ff)
        w2_new = w_full[:, :, split_at:].reshape(1, 2, n_blk, d_ff, d_model)
        mean_loss = lax.psum(loss_acc, ("stage", "data")) / n_tokens
        return w1_new, w2_new, w_new[None], m_new[None], v_new[None], mean_loss

    act_spec = P(None, "data", None)
    flat_spec = P("stage", None, None, "data")
    return jax.shard_map(device_step, mesh=mesh, in_specs=(act_spec, act_spec, P("stage"), P("stage"), flat_spec, flat_spec, flat_spec), out_specs=(P("stage"), P("stage"), flat_spec, flat_spec, flat_spec, P()), check_vma=False)
```

profile of v0, /device:TPU:0, one launch (start us, length us, event | category | flops | bytes accessed | tf_op | source)
XLA Modules:
  0.0 4649.0 jit_solution(9873661763081979653)
XLA Ops:
  7.2 32.5 broadcast_in_dim.100
  39.7 8.8 broadcast_in_dim.101
  48.6 1641.1 %while.42 = (s32[]{:T(128)}, bf16[2048,256]{1,0:T(8,128)(2,1)S(1)}, bf16[2,25,2,2048,256]{4,3,2,1,0:T(8,128)(2,1)}, bf16[25,2048,256]{2,1,0:T(8,128)(2,1)}, f32[...) while((s32[]{:T(128)}, bf16[2048,256]{1,0:T(8,128)(2,1)S(1)}, ...), condition=%wide.region_2.3_spmd, body=%wide.region_0.2_spmd.sunk | while | flops 4342677504 | bytes 23076740 | solution.py:88
  69.5 20.1 collective-permute-done
  108.9 19.6 collective-permute-done
  147.4 19.0 collective-permute-done
  185.1 18.3 collective-permute-done
  221.9 17.8 collective-permute-done
  257.9 17.2 collective-permute-done
  293.0 16.7 collective-permute-done
  327.5 15.9 collective-permute-done
  361.3 15.1 collective-permute-done
  394.3 14.1 collective-permute-done
  426.3 13.1 collective-permute-done
  457.5 12.2 collective-permute-done
  487.8 11.3 collective-permute-done
  517.4 11.0 collective-permute-done
  546.6 11.1 collective-permute-done
  575.9 11.0 collective-permute-done
  605.2 11.0 collective-permute-done
  634.5 11.0 collective-permute-done
  663.7 11.9 collective-permute-done
  693.7 13.0 collective-permute-done
  724.9 14.3 collective-permute-done
  757.2 15.4 collective-permute-done
  790.7 16.6 collective-permute-done
  825.3 17.9 collective-permute-done
  861.1 19.2 collective-permute-done
  898.0 20.4 collective-permute-done
  936.1 21.6 collective-permute-done
  975.2 22.9 collective-permute-done
  1015.7 22.1 collective-permute-done
  1055.6 21.0 collective-permute-done
  1094.7 20.0 collective-permute-done
  1133.0 18.7 collective-permute-done
  1170.5 17.5 collective-permute-done
  1206.9 16.4 collective-permute-done
  1242.5 15.5 collective-permute-done
  1277.3 14.7 collective-permute-done
  1311.2 13.8 collective-permute-done
  1344.2 13.0 collective-permute-done
  1376.4 12.2 collective-permute-done
  1407.7 11.4 collective-permute-done
  1438.4 10.4 collective-permute-done
  1468.0 9.9 collective-permute-done
  1497.2 10.0 collective-permute-done
  1526.5 10.1 collective-permute-done
  1555.9 10.0 collective-permute-done
  1585.2 10.0 collective-permute-done
  1614.5 10.6 collective-permute-done
  1644.4 9.9 collective-permute-done
  1673.7 15.9 collective-permute-done
  1694.5 2684.8 %while.43 = (s32[]{:T(128)}, bf16[2048,256]{1,0:T(8,128)(2,1)S(1)}, f32[2,2,256,1024]{3,2,1,0:T(8,128)}, f32[2,2,1024,256]{3,2,1,0:T(8,128)}, s32[]{:T(128)}, /*...) while((s32[]{:T(128)}, bf16[2048,256]{1,0:T(8,128)(2,1)S(1)}, ...), condition=%wide.region_4.5_spmd, body=%wide.region_3.4_spmd.sunk | while | flops 10864295936 | bytes 157294928 | solution.py:113
  1708.1 8.5 fusion.147
  1768.1 8.5 fusion.147
  1827.3 8.5 fusion.147
  1885.7 8.5 fusion.147
  1943.2 8.5 fusion.147
  1999.8 8.5 fusion.147
  4391.5 13.3 pad_maximum_fusion
  4406.7 144.6 %all-reduce.4.cloned.1.call-done = f32[2,2,524288]{2,1,0:T(2,128)} async-done(((f32[2,2,524288]{2,1,0:T(2,128)}), f32[2,2,524288]{2,1,0:T(2,128)}) %all-reduce.4.cloned.1.call-update) | async-done | bytes 8388624
  4555.7 23.2 all-reduce.1
  4579.6 15.4 fusion.102
  4595.7 32.8 all-gather.2.cloned.1.call-done
  (1385 shorter events, 3542.8 us)
Async XLA Ops:
  7.2 4544.2 %all-reduce.4.cloned.1.call-start = ((), (), s32[]{:S(2)}) async-start(), calls=%async_computation.1 | async-start | bytes 16777216
  63.1 26.5 collective-permute-start
  104.1 24.3 collective-permute-start
  142.9 23.5 collective-permute-start
  180.8 22.6 collective-permute-start
  217.9 21.8 collective-permute-start
  254.2 20.9 collective-permute-start
  289.6 20.1 collective-permute-start
  787.2 20.1 collective-permute-start
  821.9 21.3 collective-permute-start
  857.8 22.5 collective-permute-start
  894.8 23.6 collective-permute-start
  932.9 24.8 collective-permute-start
  972.2 25.9 collective-permute-start
  1012.6 25.2 collective-permute-start
  1052.3 24.4 collective-permute-start
  1091.2 23.5 collective-permute-start
  1129.2 22.6 collective-permute-start
  1166.3 21.7 collective-permute-start
  1202.5 20.8 collective-permute-start
  1237.8 20.2 collective-permute-start
  1668.8 20.8 collective-permute-start
  1729.0 25.8 collective-permute-start.1
  1789.1 24.9 collective-permute-start.1
  1848.3 24.1 collective-permute-start.1
  1906.6 23.2 collective-permute-start.1
  1964.1 22.4 collective-permute-start.1
  2020.7 21.5 collective-permute-start.1
  2076.5 20.6 collective-permute-start.1
  2131.4 19.8 collective-permute-start.1
  2185.5 20.4 collective-permute-start.1
  2294.1 20.4 collective-permute-start.1
  2348.8 19.8 collective-permute-start.1
  2402.8 20.4 collective-permute-start.1
  2457.4 19.7 collective-permute-start.1
  2511.4 20.4 collective-permute-start.1
  2566.1 19.8 collective-permute-start.1
  2620.1 20.4 collective-permute-start.1
  2674.8 19.7 collective-permute-start.1
  2728.7 20.4 collective-permute-start.1
  2783.4 19.8 collective-permute-start.1
  2837.4 20.4 collective-permute-start.1
  2946.1 20.4 collective-permute-start.1
  3000.7 19.8 collective-permute-start.1
  3054.7 20.4 collective-permute-start.1
  3163.4 20.4 collective-permute-start.1
  3218.0 19.8 collective-permute-start.1
  3272.1 20.4 collective-permute-start.1
  3380.7 20.4 collective-permute-start.1
  3435.4 19.8 collective-permute-start.1
  3489.4 20.4 collective-permute-start.1
  3598.0 20.4 collective-permute-start.1
  3652.7 19.8 collective-permute-start.1
  3706.7 20.4 collective-permute-start.1
  3815.4 20.4 collective-permute-start.1
  3870.0 19.8 collective-permute-start.1
  3924.0 20.4 collective-permute-start.1
  4032.7 20.4 collective-permute-start.1
  4087.3 19.8 collective-permute-start.1
  4141.4 20.4 collective-permute-start.1
  4250.0 20.4 collective-permute-start.1
  4304.7 19.8 collective-permute-start.1
  4358.7 20.4 collective-permute-start.1
  4404.8 223.6 %all-gather.2.cloned.1.call-start = ((), (), s32[]{:S(2)}) async-start(), calls=%async_computation | async-start | bytes 5242880 | tf_op jit(solution)/shard_map/all_gather | solution.py:134
  (234 other events, 3131.8 us)
Sparse Core Ops, SparseCore 0:
  4405.0 146.3 all-reduce.3
  4595.1 33.2 all-gather.1
where the time goes:
time: 4680 us; the launch traced here: 4650 us
  matrix products  3120 us (67%)
  waiting for transfers between devices  934 us (20%)
  other arithmetic  344 us (7%)
  starting transfers between devices  98.1 us (2%)
  local copies, waits for them, and re-layouts  72.7 us (2%)
    dot_general x98, matrix products, block_backward(): jnp.einsum('td,fd->tf', grad_out, w_two, preferred_element_type=jnp.float32)  784 us
    ppermute x49, waiting for transfers between devices, fwd_tick(): recv_act = lax.ppermute(h_cur, 'stage', fwd_perm)  732 us
    dot_general x98, matrix products, block_forward(): jnp.dot(act_bf, w_two, preferred_element_type=jnp.float32)  590 us
    dot_general x98, matrix products, block_backward(): pre_act = jnp.dot(h_in, w_one, preferred_element_type=jnp.float32)  579 us
    dot_general x98, matrix products, block_backward(): jnp.einsum('tf,td->fd', act_val.astype(jnp.bfloat16), grad_out, preferred...  560 us
    dot_general x98, matrix products, block_backward(): jnp.einsum('td,tf->df', h_in, grad_pre, preferred_element_type=jnp.float32)  372 us
    dot_general x98, matrix products, block_backward(): jnp.einsum('tf,df->td', grad_pre, w_one, preferred_element_type=jnp.float32)  239 us
    unnamed x3, waiting for transfers between devices  145 us
  transfers between devices with their start and end apart: 100, of which 59 were waited for; matrix products, arithmetic and copies ran while one was open for 23% of the time, Pallas kernels for 0%

commit v1 on v0

v1 whole, which is shorter than its diff:
```python
import functools
import math
import jax
import jax.numpy as jnp
from jax import lax
from jax.experimental import pallas as pl
from jax.experimental.pallas import tpu as pltpu
from jax.sharding import PartitionSpec as P

BETA_ONE = 0.9
BETA_TWO = 0.999
ADAM_EPS = 1e-8
WEIGHT_DECAY = 0.1
ADAM_STEP = 1000

ROWS = 256
CHUNK = 256
SUB = 32
NBLK = 8
SQRT_2_PI = math.sqrt(2.0 / math.pi)
F32 = jnp.float32
BF16 = jnp.bfloat16


def block_slot(b):
    return ((b // 2) % 2) * 4 + (b // 4) * 2 + b % 2


def gelu_pair(u):
    u2 = u * u
    s = jax.nn.sigmoid(u * (u2 * (2.0 * SQRT_2_PI * 0.044715) + 2.0 * SQRT_2_PI))
    a = u * s
    w = u2 * (6.0 * SQRT_2_PI * 0.044715) + 2.0 * SQRT_2_PI
    return a, s + a * ((1.0 - s) * w)


def dot(a, b):
    return jnp.dot(a, b, preferred_element_type=F32)


def dot_t(a, b):
    return lax.dot_general(a, b, (((1,), (1,)), ((), ())), preferred_element_type=F32)


def step_kernel(n_tok_inv, off_ref, x_ref, t_ref, w1_ref, w2_ref, g1_ref, g2_ref, loss_ref,
                gp_ref, a_ref, h_ref, h_cur, seed_ref, loss_acc):
    i = pl.program_id(0)

    @pl.when(i == 0)
    def _():
        seed_ref[...] = jnp.zeros_like(seed_ref)

        def clear(b, _):
            for ref in (g1_ref, g2_ref):
                ref[b] = jnp.zeros(ref.shape[1:], ref.dtype)
            for ref in (gp_ref, a_ref, h_ref):
                ref[1, b] = jnp.zeros(ref.shape[2:], ref.dtype)
            return 0

        lax.fori_loop(0, NBLK, clear, 0)
        loss_acc[...] = jnp.zeros_like(loss_acc)

    for par in range(2):
        other = 1 - par
        rows_here = slice(par * ROWS, (par + 1) * ROWS)
        h_cur[...] = x_ref[rows_here, :]

        def body(j, _, par=par, other=other):
            bb = NBLK - 1 - j
            fs = lax.rem(lax.div(j, 2), 2) * 4 + lax.div(j, 4) * 2 + lax.rem(j, 2)
            bs = lax.rem(lax.div(bb, 2), 2) * 4 + lax.div(bb, 4) * 2 + lax.rem(bb, 2)
            h = h_cur[...]
            g = seed_ref[...]
            h_ref[par, j] = h
            h_t = h_ref[other, bb].T
            g_t = g.T
            h_acc = None
            g_acc = None
            for n in range(4):
                cols = slice(n * CHUNK, (n + 1) * CHUNK)
                q = dot_t(g, w2_ref[bs, cols, :])
                u = dot(h, w1_ref[fs, :, cols])
                rs = []
                for k in range(ROWS // SUB):
                    rr = slice(k * SUB, (k + 1) * SUB)
                    rs.append((q[rr] * gp_ref[other, bb, rr, cols]).astype(BF16))
                r = jnp.concatenate(rs, axis=0)
                al = []
                for k in range(ROWS // SUB):
                    rr = slice(k * SUB, (k + 1) * SUB)
                    av, gv = gelu_pair(u[rr])
                    gp_ref[par, j, rr, cols] = gv
                    al.append(av.astype(BF16))
                a = jnp.concatenate(al, axis=0)
                a_ref[par, j, :, cols] = a
                hp = dot(a, w2_ref[fs, cols, :])
                h_acc = hp if h_acc is None else h_acc + hp
                gpart = dot_t(r, w1_ref[bs, :, cols])
                g_acc = gpart if g_acc is None else g_acc + gpart
                g1_ref[bs, :, cols] += dot(h_t, r)
                g2_ref[bs, :, cols] += dot(g_t, a_ref[other, bb, :, cols])
            h_cur[...] = (h.astype(F32) + h_acc).astype(BF16)
            seed_ref[...] = (g.astype(F32) + g_acc).astype(BF16)
            return 0

        lax.fori_loop(0, NBLK, body, 0)
        res = h_cur[...].astype(F32) - t_ref[rows_here, :].astype(F32)
        res = jnp.where(i < pl.num_programs(0) - 1, res, 0.0)
        loss_acc[...] += jnp.sum((res * res).reshape(ROWS // 8, 8, 256), axis=0)
        seed_ref[...] = (res * n_tok_inv).astype(BF16)

    @pl.when(i == pl.num_programs(0) - 1)
    def _():
        loss_ref[...] = loss_acc[...]


def run_stack(x, t, w1, w2, off, n_rows, n_tokens):
    steps = n_rows // (2 * ROWS)
    row_map = lambda i, off: (off[0] + jnp.minimum(i, steps - 1), 0)
    const3 = lambda i, off: (0, 0, 0)
    spec = pltpu.PrefetchScalarGridSpec(
        num_scalar_prefetch=1,
        grid=(steps + 1,),
        in_specs=[
            pl.BlockSpec((2 * ROWS, 256), row_map),
            pl.BlockSpec((2 * ROWS, 256), row_map),
            pl.BlockSpec((NBLK, 256, 1024), const3, pipeline_mode=pl.Buffered(1)),
            pl.BlockSpec((NBLK, 1024, 256), const3, pipeline_mode=pl.Buffered(1)),
        ],
        out_specs=[
            pl.BlockSpec((NBLK, 256, 1024), const3, pipeline_mode=pl.Buffered(1)),
            pl.BlockSpec((NBLK, 256, 1024), const3, pipeline_mode=pl.Buffered(1)),
            pl.BlockSpec((8, 256), lambda i, off: (0, 0)),
        ],
        scratch_shapes=[
            pltpu.VMEM((2, NBLK, ROWS, 1024), F32),
            pltpu.VMEM((2, NBLK, ROWS, 1024), BF16),
            pltpu.VMEM((2, NBLK, ROWS, 256), BF16),
            pltpu.VMEM((ROWS, 256), BF16),
            pltpu.VMEM((ROWS, 256), BF16),
            pltpu.VMEM((8, 256), F32),
        ],
    )
    return pl.pallas_call(
        functools.partial(step_kernel, 1.0 / n_tokens),
        grid_spec=spec,
        out_shape=[
            jax.ShapeDtypeStruct((NBLK, 256, 1024), F32),
            jax.ShapeDtypeStruct((NBLK, 256, 1024), F32),
            jax.ShapeDtypeStruct((8, 256), F32),
        ],
        compiler_params=pltpu.CompilerParams(vmem_limit_bytes=67043328),
        name="stack_step",
    )(off, x, t, w1, w2)


def adam_update(w_old, m_old, v_old, grad_val, clip_factor, learn_rate):
    grad_clip = clip_factor * grad_val
    m_new = BETA_ONE * m_old + (1.0 - BETA_ONE) * grad_clip
    v_new = BETA_TWO * v_old + (1.0 - BETA_TWO) * grad_clip * grad_clip
    m_hat = m_new / (1.0 - BETA_ONE ** ADAM_STEP)
    v_hat = v_new / (1.0 - BETA_TWO ** ADAM_STEP)
    w_new = w_old - learn_rate * (m_hat / (jnp.sqrt(v_hat) + ADAM_EPS) + WEIGHT_DECAY * w_old)
    return w_new, m_new, v_new


def solution(mesh):
    n_stage = mesh.shape["stage"]
    n_data = mesh.shape["data"]

    def device_step(x_loc, t_loc, w1_loc, w2_loc, wm_loc, m_loc, v_loc):
        n_micro, n_tok, d_model = x_loc.shape
        n_blk, d_ff = w1_loc.shape[2], w1_loc.shape[4]
        n_tokens = n_micro * n_tok * n_data
        n_blocks = 2 * n_stage * n_blk
        tau_clip = 0.3 * d_model * math.sqrt(n_blocks * (3.0 / n_tokens + 0.008))
        learn_rate = 0.1 / math.sqrt(4.0 * d_model * n_blocks)
        rows = n_micro * n_tok // n_stage
        w1 = lax.all_gather(w1_loc, "stage", axis=0, tiled=True).reshape(n_blocks, d_model, d_ff)
        w2 = lax.all_gather(w2_loc, "stage", axis=0, tiled=True).reshape(n_blocks, d_ff, d_model)
        off = (lax.axis_index("stage") * (rows // (2 * ROWS))).astype(jnp.int32).reshape(1)
        g1, g2, loss = run_stack(x_loc.reshape(-1, d_model), t_loc.reshape(-1, d_model), w1, w2, off, rows, n_tokens)
        g2 = jnp.swapaxes(g2, 1, 2)
        flat = jnp.concatenate([g1.reshape(n_stage, 2, n_blk, -1), g2.reshape(n_stage, 2, n_blk, -1)], axis=-1)
        mine = lax.psum_scatter(flat, "stage", scatter_dimension=0, tiled=True)
        grad_shard = lax.psum_scatter(mine, "data", scatter_dimension=3, tiled=True)[0]
        sums = lax.psum(jnp.stack([jnp.sum(grad_shard * grad_shard), 0.5 * jnp.sum(loss)]), ("stage", "data"))
        clip_factor = jnp.minimum(1.0, tau_clip / jnp.sqrt(sums[0]))
        w_new, m_new, v_new = adam_update(wm_loc[0], m_loc[0], v_loc[0], grad_shard, clip_factor, learn_rate)
        w_full = lax.all_gather(w_new.astype(jnp.bfloat16), "data", axis=2, tiled=True)
        split_at = d_model * d_ff
        w1_new = w_full[:, :, :split_at].reshape(1, 2, n_blk, d_model, d_ff)
        w2_new = w_full[:, :, split_at:].reshape(1, 2, n_blk, d_ff, d_model)
        return w1_new, w2_new, w_new[None], m_new[None], v_new[None], sums[1] / n_tokens

    act_spec = P(None, "data", None)
    flat_spec = P("stage", None, None, "data")
    return jax.shard_map(device_step, mesh=mesh, in_specs=(act_spec, act_spec, P("stage"), P("stage"), flat_spec, flat_spec, flat_spec), out_specs=(P("stage"), P("stage"), flat_spec, flat_spec, flat_spec, P()), check_vma=False)
```

time: 4680 us -> 2140 us (0.46)
  matrix products: 3120 us -> 0 us
  Pallas kernels: 0 us -> 1340 us
  other arithmetic: 344 us -> 49.8 us
  waiting for transfers between devices: 934 us -> 653 us
  starting transfers between devices: 98.1 us -> 0.2 us
    dot_general x588 -> x0, matrix products: 3120 us -> none  [the longest x98 784 us: block_backward(): jnp.einsum('td,fd->tf', grad_out, w_two, preferred_element_type=jnp.float32)]
    pallas_call x0 -> x1, Pallas kernels: none -> 1340 us  [run_stack(): pl.pallas_call(functools.partial(step_kernel, 1.0 / n_tokens), grid_spec=...]
    ppermute x98 -> x0, waiting for transfers between devices: 757 us -> none  [the longest x49 732 us: fwd_tick(): recv_act = lax.ppermute(h_cur, 'stage', fwd_perm)]
    unnamed x3 -> x7, waiting for transfers between devices: 145 us -> 517 us
    dynamic_update_slice x49 -> x0, other arithmetic: 120 us -> none  [fwd_tick(): lax.dynamic_update_slice(saved_in, h_cur[None, None, None], (half_idx, sl...]
    reduce_sum x49 -> x1, other arithmetic: 118 us -> 0.6 us  [device_step(): jnp.sum(loss)]
    all_gather x0 -> x2, waiting for transfers between devices: none -> 114 us  [the longest x1 57.8 us: device_step(): lax.all_gather(w1_loc, 'stage', axis=0, tiled=True)]
    ppermute x98 -> x0, starting transfers between devices: 98 us -> none  [the longest x49 50.4 us: fwd_tick(): recv_act = lax.ppermute(h_cur, 'stage', fwd_perm)]
  transfers between devices with their start and end apart: 100 -> 5, of which waited for: 59 -> 5; matrix products, arithmetic and copies ran while one was open for 23% -> 1% of each run, Pallas kernels for 0% -> 0%
where the time goes in v1:
time: 2140 us
  Pallas kernels  1340 us (63%)
  waiting for transfers between devices  653 us (31%)
  local copies, waits for them, and re-layouts  52.6 us (2%)
  other arithmetic  49.8 us (2%)
  blocking collectives  22.5 us (1%)
    pallas_call x1, Pallas kernels, run_stack(): pl.pallas_call(functools.partial(step_kernel, 1.0 / n_tokens), grid_spec=...  1340 us
    unnamed x7, waiting for transfers between devices  517 us
    all_gather x1, waiting for transfers between devices, device_step(): lax.all_gather(w1_loc, 'stage', axis=0, tiled=True)  57.8 us
    all_gather x1, waiting for transfers between devices, device_step(): lax.all_gather(w2_loc, 'stage', axis=0, tiled=True)  55.7 us
  transfers between devices with their start and end apart: 5, of which 5 were waited for; matrix products, arithmetic and copies ran while one was open for 1% of the time, Pallas kernels for 0%

profile of v1, /device:TPU:0, one launch (start us, length us, event | category | flops | bytes accessed | tf_op | source)
XLA Modules:
  0.0 2138.0 jit_solution(9553149333912341265)
XLA Ops:
  7.2 0.0 all-gather.4.cloned.1.call-start
  7.2 0.7 all-gather.4.cloned.1.call-update
  7.9 0.0 all-gather.6.cloned.1.call-start
  7.9 0.7 all-gather.6.cloned.1.call-update
  8.7 0.0 all-reduce.5.cloned.1.call-start
  8.7 57.8 %all-gather.4.cloned.1.call-done = bf16[2,2,2,256,1024]{4,3,2,1,0:T(8,128)(2,1)} async-done(((bf16[1,2,2,256,1024]{4,3,2,1,0:T(8,128)(2,1)}), bf16[2,2,2,256,1024]{4,3,2,1,0:T(8,128)(2,1)}) %all-gather.4.cloned.1.call-update) | async-done | bytes 4194320 | tf_op jit(solution)/shard_map/all_gather | solution.py:179
  66.5 55.7 %all-gather.6.cloned.1.call-done = bf16[2,2,2,1024,256]{4,3,2,1,0:T(8,128)(2,1)} async-done(((bf16[1,2,2,1024,256]{4,3,2,1,0:T(8,128)(2,1)}), bf16[2,2,2,1024,256]{4,3,2,1,0:T(8,128)(2,1)}) %all-gather.6.cloned.1.call-update) | async-done | bytes 4194320 | tf_op jit(solution)/shard_map/all_gather | solution.py:180
  122.3 1342.6 %stack_step.1 = (f32[8,256,1024]{2,1,0:T(8,128)}, f32[8,256,1024]{2,1,0:T(8,128)}, f32[8,256]{1,0:T(8,128)}) custom-call(s32[1]{0:T(128)} %bitcast.4.off_ref, bf16[49152,256]{1,0:T(8,128)(2,1)} %bitcast.46, bf16[49152,256]{1,0:T(8,128)(2,1)} %bitcast.47, bf16[8,256,1024]{2,1,0:T(8,128)(2,1)} %bitcast.49, bf16[8,1024,256]{2,1,0:T(8,128)(2,1)} %bitcast.50), custom_call_target="tpu_custom_call" | custom-call | tf_op jit(solution)/shard_map/stack_step/pallas_call | solution.py:144
  1464.9 10.8 reshape.58
  1475.7 9.1 copy.14
  1484.8 9.6 reshape.59
  1494.4 24.5 %pad_maximum_fusion = f32[2,2,2,524288]{3,2,1,0:T(2,128)} fusion(f32[2,2,2,262144]{3,2,1,0:T(2,128)} %reshape.59, f32[2,2,2,262144]{3,2,1,0:T(2,128)} %reshape.58), kind=kLoop, calls=%fused_computation | loop fusion | flops 4194304 | bytes 33554432 | tf_op jit(solution)/shard_map/concatenate | solution.py:184
  1518.9 0.0 copy-start.3
  1518.9 0.0 all-reduce.5.cloned.1.call-update
  1518.9 0.0 all-reduce.7.cloned.1.call-start
  1519.0 0.6 copy-done.3
  1519.6 0.6 dynamic-slice
  1520.2 371.1 %all-reduce.5.cloned.1.call-done = f32[2,2,2,524288]{3,2,1,0:T(2,128)} async-done(((f32[2,2,2,524288]{3,2,1,0:T(2,128)}), f32[2,2,2,524288]{3,2,1,0:T(2,128)}) %all-reduce.5.cloned.1.call-update) | async-done | bytes 16777232
  1891.2 8.0 constant_dynamic-slice_fusion
  1899.2 0.0 copy-start.2
  1899.2 0.0 copy-start.1
  1899.2 0.0 all-reduce.7.cloned.1.call-update
  1899.2 0.0 copy-start
  1899.2 0.0 all-gather.8.cloned.1.call-start
  1899.3 0.6 copy-done.2
  1899.9 0.6 dynamic-slice.2
  1901.1 0.0 copy-done.1
  1901.1 0.6 reduce_sum.19
  1902.4 144.5 %all-reduce.7.cloned.1.call-done = f32[1,2,2,524288]{3,2,1,0:T(2,128)} async-done(((f32[1,2,2,524288]{3,2,1,0:T(2,128)}), f32[1,2,2,524288]{3,2,1,0:T(2,128)}) %all-reduce.7.cloned.1.call-update) | async-done | bytes 8388624
  2046.9 4.4 multiply_reduce_fusion
  2051.2 0.7 pad_maximum_fusion.1
  2051.9 22.5 %psum.7 = f32[2]{0:T(128)S(1)} all-reduce(f32[2]{0:T(128)S(1)} %pad_maximum_fusion.1), channel_id=1, replica_groups=mesh['stage'=2,'data'=4] {'stage','data'}, use_global_device_ids=true, to_apply=%region_4.0 | all-reduce | flops 2 | bytes 16 | tf_op jit(solution)/shard_map/psum | solution.py:187
  2074.5 0.6 fusion.11
  2075.7 0.0 copy-done
  2075.8 9.2 fusion.8
  2084.9 0.0 all-gather.8.cloned.1.call-update
  2085.0 10.5 multiply_subtract_fusion
  2096.1 22.1 %all-gather.8.cloned.1.call-done = bf16[2,2,524288]{2,1,0:T(2,128)(2,1)} async-done(((bf16[2,2,131072]{2,1,0:T(2,128)(2,1)}), bf16[2,2,524288]{2,1,0:T(2,128)(2,1)}) %all-gather.8.cloned.1.call-update) | async-done | bytes 4194320 | tf_op jit(solution)/shard_map/all_gather | solution.py:190
  2118.2 5.7 fusion.10
  2123.8 3.5 reshape.61
  2127.4 3.0 reshape.60
Async XLA Ops:
  7.2 59.4 %all-gather.4.cloned.1.call-start = ((), (), s32[]{:S(2)}) async-start(), calls=%async_computation | async-start | bytes 6291456 | tf_op jit(solution)/shard_map/all_gather | solution.py:179
  7.9 114.4 %all-gather.6.cloned.1.call-start = ((), (), s32[]{:S(2)}) async-start(), calls=%async_computation.1 | async-start | bytes 6291456 | tf_op jit(solution)/shard_map/all_gather | solution.py:180
  8.7 1882.6 %all-reduce.5.cloned.1.call-start = ((), (), s32[]{:S(2)}) async-start(), calls=%async_computation.3 | async-start | bytes 33554432
  1518.9 0.7 copy-start.3
  1518.9 527.9 %all-reduce.7.cloned.1.call-start = ((), (), s32[]{:S(2)}) async-start(), calls=%async_computation.4 | async-start | bytes 16777216
  1899.2 0.7 copy-start.2
  1899.2 1.9 copy-start.1
  1899.2 176.5 %copy-start = (f32[1,2,2,131072]{3,2,1,0:T(2,128)S(1)}, f32[1,2,2,131072]{3,2,1,0:T(2,128)}, u32[]{:S(2)}) copy-start(f32[1,2,2,131072]{3,2,1,0:T(2,128)} %param.11) | copy-start | bytes 6291460
  1899.2 218.9 %all-gather.8.cloned.1.call-start = ((), (), s32[]{:S(2)}) async-start(), calls=%async_computation.2 | async-start | bytes 5242880 | tf_op jit(solution)/shard_map/all_gather | solution.py:190
Sparse Core Ops, SparseCore 0:
  9.5 57.0 all-gather.3
  68.0 54.1 all-gather.5
  1519.1 372.1 all-reduce.4
  1899.4 147.4 all-reduce.6
  2085.1 33.0 all-gather.7
